TPU v7x, 32 devices: a whole 2x2x4 slice. The times are simulated.
32 devices in a mesh: gz: 32 (over z, y, x, core).
Axes of the slice: x: 2, y: 2, z: 4, core: 2. Of those that a mesh axis runs over, the one named last changes fastest.
Arguments:
- u_face: float32 [64, 1024, 512], P('gz')
- v_face: float32 [64, 1024, 512], P('gz')
- w_face: float32 [64, 1024, 512], P('gz')
- smoke: float32 [64, 1024, 512], P('gz'), may hold values from 0 to 2
- obstacles: int32 [64, 32, 512], P('gz'), may hold values from -2147483648 to 2147483647, as said below
Outputs:
- impulse: float32 [64, 1024, 512], P('gz')
- relative_residual: float32 [64, 1024, 512], P('gz')
Inputs may be any that keep to these rules, and one draw needn't show every extreme that they name: Bit k of obstacles[z, b, x] is 1 where cell (z, 32 b + k, x) is solid and 0 where it holds fluid; every bit of a word is used.
All inputs are finite; a program needn't handle non-finite values. Where the computation divides by a largest or mean magnitude, that divisor is 1e-20 or more.
Results may differ from a plain program's by a relative error of at most 0.00011.
Values sent between devices are 32-bit elements; how exact they have to be, the bound alone decides.
A program may use at most 192 MiB of HBM per device.

v0:
```python
import jax
import jax.numpy as jnp
from jax import lax
from jax.sharding import PartitionSpec as P

ITERS = 2


EPS = 1e-06
CFL = 0.5
BUOYANCY = 100.0


def with_halo(block, sides, width):
    for axis, dim in sides:
        count = lax.axis_size(axis)
        forward = [(i, i + 1) for i in range(count - 1)]
        backward = [(target, source) for source, target in forward]
        low = lax.ppermute(
            lax.slice_in_dim(block, block.shape[dim] - width, None, axis=dim), axis, forward
        )
        high = lax.ppermute(lax.slice_in_dim(block, 0, width, axis=dim), axis, backward)
        block = jnp.concatenate([low, block, high], axis=dim)
    return block


def shifted(x, axis, by):
    devices = lax.axis_size(axis)
    pairs = [(i, i + by) for i in range(devices) if 0 <= i + by < devices]
    return lax.ppermute(x, axis, pairs)


def unpack_flags(packed):
    places = jnp.arange(32, dtype=jnp.int32)
    flags = jnp.right_shift(packed[:, :, None, :], places[None, None, :, None]) & 1
    return flags.reshape(packed.shape[0], packed.shape[1] * 32, packed.shape[2])


def later_cells(field, axis):
    size = field.shape[axis]
    tail = lax.slice_in_dim(field, 1, size, axis=axis)
    shape = list(field.shape)
    shape[axis] = 1
    return jnp.concatenate([tail, jnp.zeros(shape, field.dtype)], axis)


def earlier_cells(field, axis):
    size = field.shape[axis]
    head = lax.slice_in_dim(field, 0, size - 1, axis=axis)
    shape = list(field.shape)
    shape[axis] = 1
    return jnp.concatenate([jnp.zeros(shape, field.dtype), head], axis)


def in_plane(field):
    return (
        later_cells(field, 1)
        + earlier_cells(field, 1)
        + later_cells(field, 2)
        + earlier_cells(field, 2)
    )


def apply_operator(search, fluid_cells, solid_cells, open_count):
    masked = search * fluid_cells
    padded = with_halo(masked, (("gz", 0),), 1)
    beside_all = padded[2:] + padded[:-2] + in_plane(masked)
    return fluid_cells * (open_count * search - beside_all) + solid_cells * search


def paired_sums(residual, precond, image):
    return lax.psum((jnp.sum(residual * precond), jnp.sum(image * precond)), "gz")


def local(u_face, v_face, w_face, smoke, obstacles):
    rimmed = with_halo(obstacles, (("gz", 0),), 1)
    solid_full = unpack_flags(rimmed).astype(jnp.float32)
    solid_cells = solid_full[1:-1]
    fluid_cells = 1.0 - solid_cells
    lowest = jnp.concatenate([w_face[0:1], smoke[0:1]], 0)
    arrived = shifted(lowest, "gz", -1)
    w_next = jnp.concatenate([w_face[1:], arrived[0:1]], 0)
    smoke_next = jnp.concatenate([smoke[1:], arrived[1:2]], 0)
    around_solid = solid_full[2:] + solid_full[:-2] + in_plane(solid_cells)
    open_count = 6.0 - around_solid
    scaling = fluid_cells * jnp.maximum(open_count, 1.0) + solid_cells
    local_fastest = jnp.maximum(
        jnp.maximum(jnp.max(jnp.abs(u_face)), jnp.max(jnp.abs(v_face))), jnp.max(jnp.abs(w_face))
    )
    flat_part = later_cells(u_face, 2) - u_face + (later_cells(v_face, 1) - v_face)
    count_part = jnp.sum(fluid_cells)
    fastest = lax.pmax(local_fastest, "gz")
    time_step = CFL / (fastest + EPS)
    lift = time_step * BUOYANCY
    lifted_w = w_face + lift * smoke
    lifted_next = w_next + lift * smoke_next
    divergence = fluid_cells * (flat_part + (lifted_next - lifted_w))
    div_part = jnp.sum(divergence * divergence)
    partials = (div_part, count_part)
    totals = lax.psum((partials[0], partials[1]), "gz")
    div_squares = totals[0]
    fluid_total = jnp.maximum(totals[1], 1.0)
    residual = divergence / time_step
    solution = jnp.zeros_like(residual)
    precond = residual / scaling
    image = apply_operator(precond, fluid_cells, solid_cells, open_count)
    gamma_now, delta_now = paired_sums(residual, precond, image)
    alpha = gamma_now / delta_now
    beta_now = jnp.zeros_like(alpha)
    search = precond
    along = image
    for step in range(ITERS):
        if step > 0:
            search = precond + beta_now * search
            along = image + beta_now * along
        solution = solution + alpha * search
        residual = residual - alpha * along
        if step + 1 < ITERS:
            precond = residual / scaling
            image = apply_operator(precond, fluid_cells, solid_cells, open_count)
            gamma_next, delta_now = paired_sums(residual, precond, image)
            beta_now = gamma_next / gamma_now
            alpha = gamma_next / (delta_now - beta_now * gamma_next / alpha)
            gamma_now = gamma_next
    impulse = time_step * solution
    relative_residual = residual * time_step / jnp.sqrt(div_squares / fluid_total + EPS)
    return (impulse, relative_residual)


def solution(mesh):
    placed = (
        P("gz", None, None),
        P("gz", None, None),
        P("gz", None, None),
        P("gz", None, None),
        P("gz", None, None),
    )
    return jax.shard_map(
        local,
        mesh=mesh,
        in_specs=placed,
        out_specs=(P("gz", None, None), P("gz", None, None)),
        check_vma=False,
    )
```

profile of v0, /device:TPU:0, one launch (start us, length us, event | category | flops | bytes accessed | tf_op | source)
XLA Modules:
  0.0 392.5 jit_solution(13594354033911091391)
XLA Ops:
  0.6 0.0 copy-start.11
  0.6 6.4 %fusion.34 = (f32[1,1024,512]{2,1,0:T(8,128)}, f32[1,1024,512]{2,1,0:T(8,128)S(1)}, f32[1,1024,512]{2,1,0:T(8,128)S(1)}, f32[1,1024,512]{2,1,0:T(8,128)}) fusion(f32[2,1024,512]{2,1,0:T(8,128)} %param.7, f32[2,1024,512]{2,1,0:T(8,128)} %param.8), kind=kLoop, calls=%fused_computation.54 | loop fusion | bytes 16777216 | tf_op jit(solution)/shard_map/slice | solution.py:82
  7.1 0.0 copy-start.6
  7.1 0.0 copy-start.8
  7.1 2.6 pad_maximum_fusion.4
  9.7 1.5 collective-permute-start.2
  11.2 0.0 copy-done.11
  11.2 3.0 collective-permute-start
  14.3 0.0 copy-start.9
  14.3 1.6 collective-permute-start.1
  15.9 0.0 copy-done.6
  15.9 0.0 copy-done.8
  15.9 1.6 abs_reduce_fusion.1
  17.5 0.0 copy-done.9
  17.5 1.1 abs_reduce_fusion
  20.5 77.7 %pmax.7 = f32[]{:T(128)} all-reduce(f32[]{:T(128)S(6)} %max.15), channel_id=1, replica_groups=mesh['gz'=32] {'gz'}, use_global_device_ids=true, to_apply=%region_3.0 | all-reduce | flops 1 | bytes 8 | tf_op jit(solution)/shard_map/pmax | solution.py:92
  98.2 0.0 copy-start.7
  98.2 5.4 %slice.110 = f32[2,1024,511]{2,1,0:T(8,128)} slice(f32[2,1024,512]{2,1,0:T(8,128)} %param.5), slice={[0:2], [0:1024], [1:512]} | slice | bytes 8372224 | tf_op jit(solution)/shard_map/slice | solution.py:41
  103.6 0.0 copy-done.7
  103.6 2.5 slice.111
  106.2 0.1 shift_right_arithmetic.23
  106.8 0.0 collective-permute-done
  106.8 0.0 collective-permute-done.1
  106.9 0.9 fusion.1
  107.8 0.0 copy-start
  107.8 5.2 %fusion.27 = (f32[2,1024,511]{2,1,0:T(8,128)}, f32[2,1024,511]{2,1,0:T(8,128)}) fusion(f32[4,1024,512]{2,1,0:T(8,128)S(1)} %fusion.1), kind=kLoop, calls=%fused_computation.47 | loop fusion | bytes 16744448 | tf_op jit(solution)/shard_map/slice | solution.py:41
  112.9 0.6 copy-done
  113.5 4.3 %fusion.26 = (f32[2,1023,512]{2,1,0:T(8,128)}, f32[2,1023,512]{2,1,0:T(8,128)}) fusion(f32[4,1024,512]{2,1,0:T(8,128)S(1)} %fusion.1), kind=kLoop, calls=%fused_computation.46 | loop fusion | bytes 16760832 | tf_op jit(solution)/shard_map/slice | solution.py:41
  117.8 0.0 collective-permute-done.2
  117.8 4.0 %fusion.35 = (f32[1,1024,512]{2,1,0:T(8,128)S(1)}, f32[1,1024,512]{2,1,0:T(8,128)}) fusion(f32[2,1024,512]{2,1,0:T(8,128)} %collective-permute-done.2), kind=kLoop, calls=%fused_computation.55 | loop fusion | bytes 8388608 | tf_op jit(solution)/shard_map/slice | solution.py:82
  121.8 27.6 %fusion.19 = (f32[2,1024,512]{2,1,0:T(8,128)}, f32[2,1024,512]{2,1,0:T(8,128)}, f32[2,1024,512]{2,1,0:T(8,128)}, f32[2,1024,512]{2,1,0:T(8,128)}) fusion(f32[4,1024,512]{2,1,0:T(8,128)} %copy-done, f32[]{:T(128)S(6)} %div.34, f32[2,1024,512]{2,1,0:T(8,128)} %param.7, f32[2,1024,512]{2,1,0:T(8,128)} %param.8, f32[1,1024,512]{2,1,0:T(8,128)} %get-tuple-element.41, ...), kind=kLoop, calls=%fused_computation.43 | loop fusion | flops 26214400 | bytes 79654920 | tf_op jit(solution)/shard_map/mul | solution.py:65
  149.4 0.0 copy-start.1
  149.4 2.8 fusion.31
  152.3 1.3 collective-permute-start.3
  153.6 4.4 %collective-permute-start.4 = (f32[1,1024,512]{2,1,0:T(8,128)S(1)}, f32[1,1024,512]{2,1,0:T(8,128)}, u32[]{:S(2)}, u32[]{:S(2)}) collective-permute-start(f32[1,1024,512]{2,1,0:T(8,128)S(1)} %get-tuple-element.33), channel_id=1, source_target_pairs={{0,1},{1,2},{2,3},{3,4},{4,5},{5,6},{6,7},{7,8},{8,9},{9,10},{10,1... | collective-permute-start | bytes 6291464 | tf_op jit(solution)/shard_map/ppermute | solution.py:19
  157.9 0.0 copy-done.1
  157.9 4.8 %fusion.33 = (f32[2,1024,511]{2,1,0:T(8,128)}, f32[2,1024,511]{2,1,0:T(8,128)}) fusion(f32[2,1024,512]{2,1,0:T(8,128)S(1)} %copy-done.1), kind=kLoop, calls=%fused_computation.53 | loop fusion | bytes 16744448 | tf_op jit(solution)/shard_map/slice | solution.py:41
  162.8 4.0 %fusion.32 = (f32[2,1023,512]{2,1,0:T(8,128)}, f32[2,1023,512]{2,1,0:T(8,128)}) fusion(f32[2,1024,512]{2,1,0:T(8,128)S(1)} %copy-done.1), kind=kLoop, calls=%fused_computation.52 | loop fusion | bytes 16760832 | tf_op jit(solution)/shard_map/slice | solution.py:41
  166.8 0.0 collective-permute-done.3
  166.8 0.0 collective-permute-done.4
  166.8 16.2 %multiply_reduce_fusion.3 = (f32[]{:T(128)}, f32[]{:T(128)}, f32[2,1024,512]{2,1,0:T(8,128)}, f32[]{:T(128)}) fusion(f32[2,1024,512]{2,1,0:T(8,128)} %get-tuple-element.18, f32[2,1024,512]{2,1,0:T(8,128)} %get-tuple-element.19, f32[]{:T(128)S(6)} %div.34, f32[2,1024,511]{2,1,0:T(8,128)} %get-tuple-element.37, f32[2,1024,511]{2,1,0:T(8,128)} %get-tuple-element.36, ...), kind=kLoop, calls=%fused_computation.32 | loop fusion | flops 19922944 | bytes 46112784 | tf_op jit(solution)/shard_map/reduce_sum | solution.py:72
  183.0 75.0 %all-reduce.15 = (f32[]{:T(128)}, f32[]{:T(128)}) all-reduce(f32[]{:T(128)} %get-tuple-element.6, f32[]{:T(128)} %get-tuple-element.5), channel_id=1, replica_groups=mesh['gz'=32] {'gz'}, use_global_device_ids=true, to_apply=%region_5.0 | all-reduce | flops 2 | bytes 16 | tf_op jit(solution)/shard_map/psum | solution.py:72
  259.2 8.9 %fusion.18 = (f32[2,1024,512]{2,1,0:T(8,128)S(1)}, f32[2,1024,512]{2,1,0:T(8,128)}) fusion(f32[4,1024,512]{2,1,0:T(8,128)} %copy-done, f32[2,1024,512]{2,1,0:T(8,128)} %get-tuple-element.20, f32[2,1024,512]{2,1,0:T(8,128)} %get-tuple-element.16, f32[]{:T(128)S(6)} %div.37, f32[2,1024,512]{2,1,0:T(8,128)} %get-tuple-element.19, f32[]{:T(128)S(6)} %div.34), kind=kLoop, calls=%fused_computation.42 | loop fusion | flops 9437184 | bytes 25165832 | tf_op jit(solution)/shard_map/mul | solution.py:65
  268.1 2.4 fusion.28
  270.5 1.3 collective-permute-start.5
  271.8 4.3 %collective-permute-start.6 = (f32[1,1024,512]{2,1,0:T(8,128)}, f32[1,1024,512]{2,1,0:T(8,128)}, u32[]{:S(2)}, u32[]{:S(2)}) collective-permute-start(f32[1,1024,512]{2,1,0:T(8,128)} %get-tuple-element.27), channel_id=1, source_target_pairs={{0,1},{1,2},{2,3},{3,4},{4,5},{5,6},{6,7},{7,8},{8,9},{9,10},{10,1... | collective-permute-start | bytes 6291464 | tf_op jit(solution)/shard_map/ppermute | solution.py:19
  276.1 4.8 %fusion.30 = (f32[2,1024,511]{2,1,0:T(8,128)}, f32[2,1024,511]{2,1,0:T(8,128)}) fusion(f32[2,1024,512]{2,1,0:T(8,128)S(1)} %get-tuple-element.14), kind=kLoop, calls=%fused_computation.50 | loop fusion | bytes 16744448 | tf_op jit(solution)/shard_map/slice | solution.py:41
  280.9 4.9 %fusion.29 = (f32[2,1023,512]{2,1,0:T(8,128)}, f32[2,1023,512]{2,1,0:T(8,128)}) fusion(f32[2,1024,512]{2,1,0:T(8,128)S(1)} %get-tuple-element.14), kind=kLoop, calls=%fused_computation.49 | loop fusion | bytes 16760832 | tf_op jit(solution)/shard_map/slice | solution.py:41
  285.8 0.0 collective-permute-done.5
  285.8 0.0 collective-permute-done.6
  285.8 0.0 slice-done
  285.8 0.0 slice-done.1
  285.8 1.4 copy-done.2
  287.3 1.2 copy-done.4
  288.5 13.7 %multiply_reduce_fusion = (f32[]{:T(128)}, f32[]{:T(128)}, f32[]{:T(128)}, f32[2,1024,512]{2,1,0:T(8,128)}) fusion(f32[2,1024,512]{2,1,0:T(8,128)S(1)} %copy-done.2, f32[2,1024,512]{2,1,0:T(8,128)} %get-tuple-element.15, f32[2,1024,512]{2,1,0:T(8,128)S(1)} %copy-done.4, f32[]{:T(128)S(6)} %div.37, f32[]{:T(128)S(6)} %div.34, ...), kind=kLoop, calls=%fused_computation.26 | loop fusion | flops 23068668 | bytes 50307092 | tf_op jit(solution)/shard_map/reduce_sum | solution.py:98
  302.2 73.1 %all-reduce.14 = (f32[]{:T(128)}, f32[]{:T(128)}, f32[]{:T(128)}, f32[]{:T(128)}) all-reduce(f32[]{:T(128)} %get-tuple-element.3, f32[]{:T(128)} %get-tuple-element.4, f32[]{:T(128)} %get-tuple-element.2, f32[]{:T(128)} %get-tuple-element.21), channel_id=1, replica_groups=mesh['gz'=32] {'gz'}, use_global_device_ids=true, to_apply=%region_9.0 | all-reduce | flops 4 | bytes 32 | tf_op jit(solution)/shard_map/psum | solution.py:72
  380.9 0.0 copy-start.3
  380.9 0.0 copy-start.5
  380.9 0.0 copy-start.10
  380.9 6.9 %add_multiply_fusion = f32[2,1024,512]{2,1,0:T(8,128)} fusion(f32[2,1024,512]{2,1,0:T(8,128)} %get-tuple-element.15, f32[2,1024,512]{2,1,0:T(8,128)} %get-tuple-element.18, f32[]{:T(128)S(6)} %div.39, f32[]{:T(128)S(6)} %div.41, f32[]{:T(128)S(6)} %div.37, f32[]{:T(128)S(6)} %div.34), kind=kLoop, calls=%fused_computation.28 | loop fusion | flops 6291456 | bytes 12582928 | tf_op jit(solution)/shard_map/mul | solution.py:125
  387.8 0.0 copy-done.3
  387.8 0.0 copy-done.5
  387.8 1.7 copy-done.10
  389.6 3.0 multiply_divide_fusion
  (8 shorter events, 0.0 us)
Async XLA Ops:
  0.6 10.6 %copy-start.11 = (s32[2,32,512]{2,1,0:T(8,128)S(1)}, s32[2,32,512]{2,1,0:T(8,128)}, u32[]{:S(2)}) copy-start(s32[2,32,512]{2,1,0:T(8,128)} %param.9) | copy-start | bytes 393220
  7.1 8.8 %copy-start.6 = (f32[2,1024,512]{2,1,0:T(8,128)S(1)}, f32[2,1024,512]{2,1,0:T(8,128)}, u32[]{:S(2)}) copy-start(f32[2,1024,512]{2,1,0:T(8,128)} %param.6) | copy-start | bytes 12582916
  7.1 8.8 %copy-start.8 = (f32[2,1024,512]{2,1,0:T(8,128)S(1)}, f32[2,1024,512]{2,1,0:T(8,128)}, u32[]{:S(2)}) copy-start(f32[2,1024,512]{2,1,0:T(8,128)} %param.5) | copy-start | bytes 12582916
  9.7 108.1 %collective-permute-start.2 = (f32[2,1024,512]{2,1,0:T(8,128)}, f32[2,1024,512]{2,1,0:T(8,128)}, u32[]{:S(2)}, u32[]{:S(2)}) collective-permute-start(f32[2,1024,512]{2,1,0:T(8,128)} %pad_maximum_fusion.4), channel_id=1, source_target_pairs={{1,0},{2,1},{3,2},{4,3},{5,4},{6,5},{7,6},{8,7},{9,8},{10,9},{11,1... | collective-permute-start | bytes 12582920 | tf_op jit(solution)/shard_map/ppermute | solution.py:30
  11.2 95.6 %collective-permute-start = (s32[1,32,512]{2,1,0:T(8,128)S(1)}, s32[1,32,512]{2,1,0:T(8,128)S(1)}, u32[]{:S(2)}, u32[]{:S(2)}) collective-permute-start(s32[1,32,512]{2,1,0:T(8,128)S(1)} %get-tuple-element.44), channel_id=1, source_target_pairs={{0,1},{1,2},{2,3},{3,4},{4,5},{5,6},{6,7},{7,8},{8,9},{9,10},{10,1... | collective-permute-start | bytes 196616 | tf_op jit(solution)/shard_map/ppermute | solution.py:19
  14.3 3.2 copy-start.9
  14.3 92.5 %collective-permute-start.1 = (s32[1,32,512]{2,1,0:T(8,128)S(1)}, s32[1,32,512]{2,1,0:T(8,128)S(1)}, u32[]{:S(2)}, u32[]{:S(2)}) collective-permute-start(s32[1,32,512]{2,1,0:T(8,128)S(1)} %get-tuple-element.45), channel_id=1, source_target_pairs={{1,0},{2,1},{3,2},{4,3},{5,4},{6,5},{7,6},{8,7},{9,8},{10,9},{11,1... | collective-permute-start | bytes 196616 | tf_op jit(solution)/shard_map/ppermute | solution.py:22
  98.2 5.4 %copy-start.7 = (f32[2,1024,512]{2,1,0:T(8,128)S(1)}, f32[2,1024,512]{2,1,0:T(8,128)}, u32[]{:S(2)}) copy-start(f32[2,1024,512]{2,1,0:T(8,128)} %param.6) | copy-start | bytes 12582916
  107.8 5.8 %copy-start = (f32[4,1024,512]{2,1,0:T(8,128)}, f32[4,1024,512]{2,1,0:T(8,128)S(1)}, u32[]{:S(2)}) copy-start(f32[4,1024,512]{2,1,0:T(8,128)S(1)} %fusion.1) | copy-start | bytes 25165828
  149.4 8.5 %copy-start.1 = (f32[2,1024,512]{2,1,0:T(8,128)S(1)}, f32[2,1024,512]{2,1,0:T(8,128)}, u32[]{:S(2)}) copy-start(f32[2,1024,512]{2,1,0:T(8,128)} %get-tuple-element.17) | copy-start | bytes 12582916
  152.3 14.5 %collective-permute-start.3 = (f32[1,1024,512]{2,1,0:T(8,128)S(1)}, f32[1,1024,512]{2,1,0:T(8,128)S(1)}, u32[]{:S(2)}, u32[]{:S(2)}) collective-permute-start(f32[1,1024,512]{2,1,0:T(8,128)S(1)} %get-tuple-element.32), channel_id=1, source_target_pairs={{1,0},{2,1},{3,2},{4,3},{5,4},{6,5},{7,6},{8,7},{9,8},{10,9},{11,1... | collective-permute-start | bytes 6291464 | tf_op jit(solution)/shard_map/ppermute | solution.py:22
  153.6 13.2 %collective-permute-start.4 = (f32[1,1024,512]{2,1,0:T(8,128)S(1)}, f32[1,1024,512]{2,1,0:T(8,128)}, u32[]{:S(2)}, u32[]{:S(2)}) collective-permute-start(f32[1,1024,512]{2,1,0:T(8,128)S(1)} %get-tuple-element.33), channel_id=1, source_target_pairs={{0,1},{1,2},{2,3},{3,4},{4,5},{5,6},{6,7},{7,8},{8,9},{9,10},{10,1... | collective-permute-start | bytes 6291464 | tf_op jit(solution)/shard_map/ppermute | solution.py:19
  270.5 15.4 %collective-permute-start.5 = (f32[1,1024,512]{2,1,0:T(8,128)}, f32[1,1024,512]{2,1,0:T(8,128)}, u32[]{:S(2)}, u32[]{:S(2)}) collective-permute-start(f32[1,1024,512]{2,1,0:T(8,128)} %get-tuple-element.26), channel_id=1, source_target_pairs={{1,0},{2,1},{3,2},{4,3},{5,4},{6,5},{7,6},{8,7},{9,8},{10,9},{11,1... | collective-permute-start | bytes 6291464 | tf_op jit(solution)/shard_map/ppermute | solution.py:22
  271.8 14.1 %collective-permute-start.6 = (f32[1,1024,512]{2,1,0:T(8,128)}, f32[1,1024,512]{2,1,0:T(8,128)}, u32[]{:S(2)}, u32[]{:S(2)}) collective-permute-start(f32[1,1024,512]{2,1,0:T(8,128)} %get-tuple-element.27), channel_id=1, source_target_pairs={{0,1},{1,2},{2,3},{3,4},{4,5},{5,6},{6,7},{7,8},{8,9},{9,10},{10,1... | collective-permute-start | bytes 6291464 | tf_op jit(solution)/shard_map/ppermute | solution.py:19
  276.1 9.7 %slice-start = ((s8[8388608]{0:T(1024)(128)(4,1)}), s8[4194304]{0:T(1024)(128)(4,1)S(1)}, s32[]{:S(2)}) async-start(s8[8388608]{0:T(1024)(128)(4,1)} %bitcast.6), calls=%async_computation | async-start | bytes 8388608
  280.9 4.9 %slice-start.1 = ((s8[8388608]{0:T(1024)(128)(4,1)}), s8[4194304]{0:T(1024)(128)(4,1)S(1)}, s32[]{:S(2)}) async-start(s8[8388608]{0:T(1024)(128)(4,1)} %bitcast.6), calls=%async_computation.1 | async-start | bytes 8388608
  280.9 6.4 %copy-start.2 = (f32[2,1024,512]{2,1,0:T(8,128)S(1)}, f32[2,1024,512]{2,1,0:T(8,128)}, u32[]{:S(2)}) copy-start(f32[2,1024,512]{2,1,0:T(8,128)} %get-tuple-element.19) | copy-start | bytes 12582916
  280.9 7.6 %copy-start.4 = (f32[2,1024,512]{2,1,0:T(8,128)S(1)}, f32[2,1024,512]{2,1,0:T(8,128)}, u32[]{:S(2)}) copy-start(f32[2,1024,512]{2,1,0:T(8,128)} %get-tuple-element.16) | copy-start | bytes 12582916
  380.9 6.9 %copy-start.3 = (f32[2,1024,512]{2,1,0:T(8,128)S(1)}, f32[2,1024,512]{2,1,0:T(8,128)}, u32[]{:S(2)}) copy-start(f32[2,1024,512]{2,1,0:T(8,128)} %get-tuple-element.19) | copy-start | bytes 12582916
  380.9 6.9 %copy-start.5 = (f32[2,1024,512]{2,1,0:T(8,128)S(1)}, f32[2,1024,512]{2,1,0:T(8,128)}, u32[]{:S(2)}) copy-start(f32[2,1024,512]{2,1,0:T(8,128)} %get-tuple-element.16) | copy-start | bytes 12582916
  380.9 8.6 %copy-start.10 = (f32[2,1024,512]{2,1,0:T(8,128)S(1)}, f32[2,1024,512]{2,1,0:T(8,128)}, u32[]{:S(2)}) copy-start(f32[2,1024,512]{2,1,0:T(8,128)} %get-tuple-element.13) | copy-start | bytes 12582916
where the time goes:
time: 393 us
  blocking collectives  226 us (58%)
  other arithmetic  82.4 us (21%)
  local copies, waits for them, and re-layouts  56.7 us (14%)
  starting transfers between devices  17.4 us (4%)
  between operations  10.3 us (3%)
    psum x2, blocking collectives, paired_sums(): lax.psum((jnp.sum(residual * precond), jnp.sum(image * precond)), 'gz')  148 us
    pmax x1, blocking collectives, local(): fastest = lax.pmax(local_fastest, 'gz')  77.7 us
    mul x2, other arithmetic, apply_operator(): masked = search * fluid_cells  36.5 us
    slice x8, local copies, waits for them, and re-layouts, later_cells(): tail = lax.slice_in_dim(field, 1, size, axis=axis)  36 us
    reduce_sum x1, other arithmetic, paired_sums(): jnp.sum(image * precond)  16.2 us
    reduce_sum x1, other arithmetic, local(): div_part = jnp.sum(divergence * divergence)  13.7 us
    ppermute x3, starting transfers between devices, with_halo(): lax.ppermute(lax.slice_in_dim(block, block.shape[dim] - width, None, axis...  11.8 us
    slice x2, local copies, waits for them, and re-layouts, local(): w_next = jnp.concatenate([w_face[1:], arrived[0:1]], 0)  10.5 us
  transfers between devices with their start and end apart: 7, of which 0 were waited for; matrix products, arithmetic and copies ran while one was open for 10% of the time, Pallas kernels for 0%

commit v1 on v0

v1 whole, which is shorter than its diff:
```python
import functools

import jax
import jax.numpy as jnp
from jax import lax
from jax.experimental import pallas as pl
from jax.experimental.pallas import tpu as pltpu
from jax.sharding import PartitionSpec as P

EPS = 1e-06
CFL = 0.5
BUOYANCY = 100.0

ROWS = 32
PAD = 8


def kernel(n, chunks, u_hbm, v_hbm, w_hbm, s_hbm, ob_hbm, imp_hbm, res_hbm,
           u, v, w, s, z, y, code, ay, lw, lw_next, ob, cw, acc, cf, mx, mx_all, st, st_all,
           in_sem, ob_send, ob_recv, lw_send, lw_recv, dn_send, dn_recv, up_send, up_recv,
           mx_send, mx_recv, st_send, st_recv, out_sem):
    depth, ny, nx = w.shape
    nb = ny // ROWS
    crow = ny // chunks
    me = lax.axis_index("gz")
    has_low, has_high = me > 0, me < n - 1
    low, high = jnp.maximum(me - 1, 0), jnp.minimum(me + 1, n - 1)

    def at(device):
        return dict(device_id=(device,), device_id_type=pl.DeviceIdType.MESH)

    ins = [(u_hbm, u), (v_hbm, v), (w_hbm, w), (s_hbm, s)]

    def load(k, p):
        src, dst = ins[k]
        return pltpu.make_async_copy(src.at[p], dst.at[p, pl.ds(0, ny)], in_sem.at[k * depth + p])

    ob_in = pltpu.make_async_copy(ob_hbm, ob.at[pl.ds(2, depth)], in_sem.at[4 * depth])
    ob_in.start()
    for k in range(4):
        for p in range(depth):
            load(k, p).start()

    barrier = pltpu.get_barrier_semaphore()

    def greet(i, carry):
        pl.semaphore_signal(barrier, inc=1, **at(lax.rem(me + i, n)))
        return carry

    lax.fori_loop(1, n, greet, 0)

    zrow = jnp.zeros((PAD, nx), jnp.float32)
    for p in range(depth + 4):
        z[p, 0:PAD, :] = zrow
        z[p, ny + PAD : ny + 2 * PAD, :] = zrow
    for p in range(depth + 2):
        y[p, 0:PAD, :] = zrow
        y[p, ny + PAD : ny + 2 * PAD, :] = zrow
    for p in range(depth):
        v[p, ny : ny + PAD, :] = zrow
    acc[...] = jnp.zeros_like(acc)

    def zero_planes(ref, planes, offset):
        def body(i, carry):
            for p in planes:
                ref[p, pl.ds(pl.multiple_of(i * ROWS + offset, 8), ROWS), :] = jnp.zeros((ROWS, nx), jnp.float32)
            return carry
        lax.fori_loop(0, nb, body, 0)

    ob_in.wait()
    pl.semaphore_wait(barrier, n - 1)

    ob_down = pltpu.make_async_remote_copy(
        ob.at[pl.ds(2, 2)], ob.at[pl.ds(depth + 2, 2)], ob_send.at[0], ob_recv.at[0], **at(low))
    ob_up = pltpu.make_async_remote_copy(
        ob.at[pl.ds(depth, 2)], ob.at[pl.ds(0, 2)], ob_send.at[1], ob_recv.at[1], **at(high))

    @pl.when(has_low)
    def _():
        ob_down.start()

    @pl.when(has_high)
    def _():
        ob_up.start()

    @pl.when(jnp.logical_not(has_low))
    def _():
        ob[0:2] = jnp.zeros((2,) + ob.shape[1:], jnp.int32)
        zero_planes(z, (0, 1), PAD)

    @pl.when(jnp.logical_not(has_high))
    def _():
        ob[depth + 2 : depth + 4] = jnp.zeros((2,) + ob.shape[1:], jnp.int32)
        zero_planes(z, (depth + 2, depth + 3), PAD)
        zero_planes(lw_next, (0,), 0)

    mx[...] = jnp.zeros_like(mx)
    for k in range(3):
        ref = ins[k][1]
        for p in range(depth):
            load(k, p).wait()

            def body(i, m, ref=ref, p=p):
                a = jnp.abs(ref[p, pl.ds(pl.multiple_of(i * ROWS, 8), ROWS), :])
                return jnp.maximum(m, jnp.max(a.reshape(ROWS // 8, 8, nx), axis=0))

            m = lax.fori_loop(0, nb, body, jnp.zeros((8, nx), jnp.float32))
            m = jnp.max(m, axis=0, keepdims=True)
            for c in range(0, nx, 128):
                mx[...] = jnp.maximum(mx[...], jnp.broadcast_to(m[:, c : c + 128], mx.shape))

    def spread(src, dst, send, recv):
        def copy(i):
            return pltpu.make_async_remote_copy(
                src, dst.at[i], send.at[i], recv.at[i], **at(lax.rem(me + i, n)))

        def start(i, carry):
            copy(i).start()
            return carry

        def wait(i, carry):
            copy(i).wait_recv()
            copy(i).wait_send()
            return carry

        return (lambda: lax.fori_loop(1, n, start, 0)), (lambda: lax.fori_loop(1, n, wait, 0))

    mx_start, mx_wait = spread(mx, mx_all, mx_send, mx_recv)
    mx_start()

    @pl.when(has_low)
    def _():
        ob_down.wait_send()
        ob_up.wait_recv()

    @pl.when(has_high)
    def _():
        ob_up.wait_send()
        ob_down.wait_recv()

    row_id = lax.broadcasted_iota(jnp.int32, (nb, nx), 0)
    col_id = lax.broadcasted_iota(jnp.int32, (nb, nx), 1)
    srl = lax.shift_right_logical
    c1, c31 = jnp.int32(1), jnp.int32(31)
    full1, full31 = jnp.full((nb, nx), c1), jnp.full((nb, nx), c31)
    for p in range(depth + 2):
        mid = ob[p + 1]
        after = jnp.where(row_id == nb - 1, 0, pltpu.roll(mid, nb - 1, 0))
        before = jnp.where(row_id == 0, 0, pltpu.roll(mid, 1, 0))
        a = srl(mid, full1) | (after << full31)
        b = (mid << full1) | srl(before, full31)
        c = jnp.where(col_id == nx - 1, 0, pltpu.roll(mid, nx - 1, 1))
        d = jnp.where(col_id == 0, 0, pltpu.roll(mid, 1, 1))
        e, f = ob[p], ob[p + 2]
        s1, k1 = a ^ b ^ c, (a & b) | (c & (a | b))
        s2, k2 = d ^ e ^ f, (d & e) | (f & (d | e))
        k3 = s1 & s2
        cw[p, 0] = s1 ^ s2
        cw[p, 1] = k1 ^ k2 ^ k3
        cw[p, 2] = (k1 & k2) | (k3 & (k1 | k2))
        outside = None
        if p == 0:
            outside = jnp.logical_not(has_low)
        if p == depth + 1:
            outside = jnp.logical_not(has_high)
        cw[p, 3] = mid
        if outside is not None:
            @pl.when(outside)
            def _(p=p):
                cw[p, 3] = jnp.full((nb, nx), -1, jnp.int32)

    half = 16
    places = lax.broadcasted_iota(jnp.int32, (half, nx), 0)

    def code_rows(b, carry):
        for p in range(depth + 2):
            for k0 in range(0, ROWS, half):
                bits = [
                    srl(jnp.broadcast_to(cw[p, j, pl.ds(b, 1), :], (half, nx)), places + k0) & 1
                    for j in range(4)
                ]
                count = bits[0] + (bits[1] << 1) + (bits[2] << 2)
                code[p, pl.ds(pl.multiple_of(b * ROWS + k0, 8), half), :] = jnp.where(
                    bits[3] == 1, -1, 6 - count).astype(jnp.float32)
        return carry

    lax.fori_loop(0, nb, code_rows, 0)

    for p in range(depth):
        load(3, p).wait()
    mx_wait()
    mx_all[0] = mx[...]
    top = jnp.max(jnp.max(mx_all[...], axis=0), axis=1, keepdims=True)[0:1]
    top = jnp.broadcast_to(top, (1, nx))
    cf[0:1, :] = (CFL / (top + EPS)) * BUOYANCY

    lane = lax.broadcasted_iota(jnp.int32, (ROWS, nx), 1)

    def lifted(p, r):
        rows = pl.ds(r, ROWS)
        return w[p, rows, :] + cf[0:1, :] * s[p, rows, :]

    def chunked(prepare, compute, sends):
        def body(c, carry):
            @pl.when(c < chunks)
            def _():
                prepare(c)

                def inner(i, k):
                    compute(pl.multiple_of(c * crow + i * ROWS, 8))
                    return k
                lax.fori_loop(0, crow // ROWS, inner, 0)

            @pl.when(c > 0)
            def _():
                for cond, copy in sends:
                    @pl.when(cond)
                    def _(copy=copy):
                        copy(c - 1).start()
            return carry
        lax.fori_loop(0, chunks + 1, body, 0)

    def lw_copy(c):
        rows = pl.ds(pl.multiple_of(c * crow, 8), crow)
        return pltpu.make_async_remote_copy(
            lw.at[0, rows], lw_next.at[0, rows], lw_send.at[c], lw_recv.at[c], **at(low))

    def lw_rows(r):
        lw[0, pl.ds(r, ROWS), :] = lifted(0, r)

    chunked(lambda c: None, lw_rows, [(has_low, lw_copy)])

    def z_copy(src, dst, send, recv, base, device):
        def copy(c):
            rows = pl.ds(pl.multiple_of(c * crow + PAD, 8), crow)
            return pltpu.make_async_remote_copy(
                z.at[src, rows], z.at[dst, rows], send.at[base + c], recv.at[base + c], **at(device))
        return copy

    down = [z_copy(2 + j, depth + 2 + j, dn_send, dn_recv, j * chunks, low) for j in range(2)]
    up = [z_copy(depth + j, j, up_send, up_recv, j * chunks, high) for j in range(2)]

    def z_rows(p, r):
        rows = pl.ds(r, ROWS)
        a = u[p, rows, :]
        flat = jnp.where(lane == nx - 1, 0.0, pltpu.roll(a, nx - 1, 1)) - a
        b = v[p, pl.ds(r, ROWS + PAD), :]
        flat = flat + (b[1 : ROWS + 1] - b[:ROWS])
        above = lifted(p + 1, r) if p + 1 < depth else lw_next[0, rows, :]
        own = lw[0, rows, :] if p == 0 else lifted(p, r)
        div = flat + (above - own)
        k = code[p + 1, rows, :]
        z[p + 2, pl.ds(pl.multiple_of(r + PAD, 8), ROWS), :] = (
            jnp.where(k >= 0.0, div, 0.0) / jnp.maximum(k, 1.0))

    for p in range(depth):
        def prepare(c, p=p):
            if p == depth - 1:
                @pl.when(has_high)
                def _():
                    lw_copy(c).wait_recv()
        sends = []
        if p < 2:
            sends.append((has_low, down[p]))
        if p >= depth - 2:
            sends.append((has_high, up[p - (depth - 2)]))
        chunked(prepare, functools.partial(z_rows, p), sends)

    def wait_all(cond, copy):
        def body(c, carry):
            @pl.when(cond)
            def _():
                copy(c).wait_recv()
            return carry
        lax.fori_loop(0, chunks, body, 0)

    def image(ref, slot, zm, zp, r, k):
        x = ref[slot, pl.ds(r, ROWS + 2 * PAD), :]
        mid = x[PAD : PAD + ROWS]
        beside = x[PAD + 1 : PAD + 1 + ROWS] + x[PAD - 1 : PAD - 1 + ROWS]
        beside = beside + jnp.where(lane == nx - 1, 0.0, pltpu.roll(mid, nx - 1, 1))
        beside = beside + jnp.where(lane == 0, 0.0, pltpu.roll(mid, 1, 1))
        beside = beside + zm + zp
        return mid, jnp.where(k >= 0.0, k * mid - beside, mid)

    def add(j, x):
        acc[j] += jnp.sum(x.reshape(ROWS // 8, 8, nx), axis=0)

    def y_rows(p, r):
        inner = pl.ds(pl.multiple_of(r + PAD, 8), ROWS)
        k = code[p + 1, pl.ds(r, ROWS), :]
        mid, q = image(z, p + 2, z[p + 1, inner, :], z[p + 3, inner, :], r, k)
        scaling = jnp.maximum(k, 1.0)
        out = q / scaling
        y[p + 1, inner, :] = out
        if 0 <= p < depth:
            d = scaling * mid
            add(0, d * mid)
            add(1, d * d)
            add(2, jnp.where(k >= 0.0, 1.0, 0.0))
            add(3, mid * q)
            add(4, q * out)

    def a_rows(p, r):
        inner = pl.ds(pl.multiple_of(r + PAD, 8), ROWS)
        k = code[p + 1, pl.ds(r, ROWS), :]
        mid, q = image(y, p + 1, y[p, inner, :], y[p + 2, inner, :], r, k)
        ay[p, pl.ds(r, ROWS), :] = q
        add(5, mid * q)

    def sweep(fn):
        def body(i, carry):
            fn(pl.multiple_of(i * ROWS, 8))
            return carry
        lax.fori_loop(0, nb, body, 0)

    wait_all(has_low, up[0])
    for p in range(depth - 1):
        if p == 0:
            wait_all(has_low, up[1])
            sweep(functools.partial(y_rows, -1))
        sweep(functools.partial(y_rows, p))
    wait_all(has_high, down[0])
    sweep(functools.partial(y_rows, depth - 1))
    for p in range(depth - 1):
        sweep(functools.partial(a_rows, p))

    def last_wait(c):
        @pl.when(has_high)
        def _():
            down[1](c).wait_recv()

    def last_rows(r):
        y_rows(depth, r)
        a_rows(depth - 1, r)

    chunked(last_wait, last_rows, [])

    for j in range(6):
        t = jnp.sum(acc[j], axis=0, keepdims=True)
        part = t[:, 0:128]
        for c in range(128, nx, 128):
            part = part + t[:, c : c + 128]
        st[j : j + 1, :] = part
    st[6:8, :] = jnp.zeros((2, 128), jnp.float32)
    st_start, st_wait = spread(st, st_all, st_send, st_recv)
    st_start()

    def drain(c, carry):
        @pl.when(has_low)
        def _():
            lw_copy(c).wait_send()
            down[0](c).wait_send()
            down[1](c).wait_send()

        @pl.when(has_high)
        def _():
            up[0](c).wait_send()
            up[1](c).wait_send()
        return carry

    lax.fori_loop(0, chunks, drain, 0)
    st_wait()
    st_all[0] = st[...]
    total = jnp.sum(jnp.sum(st_all[...], axis=0), axis=1, keepdims=True)
    total = jnp.broadcast_to(total, (8, nx))
    gamma, squares, fluid = total[0:1], total[1:2], total[2:3]
    delta, eta, theta = total[3:4], total[4:5], total[5:6]
    alpha = gamma / delta
    gamma_next = gamma - 2.0 * alpha * delta + alpha * alpha * eta
    beta = gamma_next / gamma
    mixed = delta - alpha * eta
    curve = (delta - 2.0 * alpha * eta + alpha * alpha * theta) + 2.0 * beta * mixed + beta * beta * delta
    alpha_next = gamma_next / curve
    cf[1:2, :] = alpha + alpha_next * (1.0 + beta)
    cf[2:3, :] = alpha * alpha_next
    cf[3:4, :] = 1.0 / jnp.sqrt(squares / jnp.maximum(fluid, 1.0) + EPS)

    def out_copy(p, c, j):
        rows = pl.ds(pl.multiple_of(c * crow, 8), crow)
        src, dst = ((w, imp_hbm), (s, res_hbm))[j]
        return pltpu.make_async_copy(src.at[p, rows], dst.at[p, rows], out_sem.at[j * depth + p, c])

    for p in range(depth):
        def out_rows(r, p=p):
            inner = pl.ds(pl.multiple_of(r + PAD, 8), ROWS)
            rows = pl.ds(r, ROWS)
            zz, yy = z[p + 2, inner, :], y[p + 1, inner, :]
            scaling = jnp.maximum(code[p + 1, rows, :], 1.0)
            a, b = cf[1:2, :], cf[2:3, :]
            w[p, rows, :] = a * zz - b * yy
            s[p, rows, :] = (scaling * (zz - a * yy) + b * ay[p, rows, :]) * cf[3:4, :]

        chunked(lambda c: None, out_rows,
                [(True, lambda c, p=p: out_copy(p, c, 0)), (True, lambda c, p=p: out_copy(p, c, 1))])

    def finish(c, carry):
        for p in range(depth):
            for j in range(2):
                out_copy(p, c, j).wait()
        return carry

    lax.fori_loop(0, chunks, finish, 0)


def solution(mesh):
    n = mesh.shape["gz"]

    def local(u_face, v_face, w_face, smoke, obstacles):
        depth, ny, nx = u_face.shape
        nw = obstacles.shape[1]
        chunks = 8
        f32, i32 = jnp.float32, jnp.int32
        dma = pltpu.SemaphoreType.DMA
        any_spec = pl.BlockSpec(memory_space=pl.ANY)
        shape = jax.ShapeDtypeStruct((depth, ny, nx), f32)
        return pl.pallas_call(
            functools.partial(kernel, n, chunks),
            out_shape=(shape, shape),
            in_specs=[any_spec] * 5,
            out_specs=(any_spec, any_spec),
            scratch_shapes=[
                pltpu.VMEM((depth, ny, nx), f32),
                pltpu.VMEM((depth, ny + PAD, nx), f32),
                pltpu.VMEM((depth, ny, nx), f32),
                pltpu.VMEM((depth, ny, nx), f32),
                pltpu.VMEM((depth + 4, ny + 2 * PAD, nx), f32),
                pltpu.VMEM((depth + 2, ny + 2 * PAD, nx), f32),
                pltpu.VMEM((depth + 2, ny, nx), f32),
                pltpu.VMEM((depth, ny, nx), f32),
                pltpu.VMEM((1, ny, nx), f32),
                pltpu.VMEM((1, ny, nx), f32),
                pltpu.VMEM((depth + 4, nw, nx), i32),
                pltpu.VMEM((depth + 2, 4, nw, nx), i32),
                pltpu.VMEM((6, 8, nx), f32),
                pltpu.VMEM((8, nx), f32),
                pltpu.VMEM((8, 128), f32),
                pltpu.VMEM((n, 8, 128), f32),
                pltpu.VMEM((8, 128), f32),
                pltpu.VMEM((n, 8, 128), f32),
                dma((4 * depth + 1,)),
                dma((2,)), dma((2,)),
                dma((chunks,)), dma((chunks,)),
                dma((2 * chunks,)), dma((2 * chunks,)),
                dma((2 * chunks,)), dma((2 * chunks,)),
                dma((n,)), dma((n,)),
                dma((n,)), dma((n,)),
                dma((2 * depth, chunks)),
            ],
            compiler_params=pltpu.CompilerParams(
                collective_id=0, has_side_effects=True, vmem_limit_bytes=66_000_000),
            name="smoke_step",
        )(u_face, v_face, w_face, smoke, obstacles)

    placed = P("gz", None, None)
    return jax.shard_map(local, mesh=mesh, in_specs=(placed,) * 5, out_specs=(placed, placed), check_vma=False)
```

time: 393 us -> 174 us (0.44)
  blocking collectives: 226 us -> 0 us
  Pallas kernels: 0 us -> 166 us
  other arithmetic: 82.4 us -> 0 us
  local copies, waits for them, and re-layouts: 56.7 us -> 6.84 us
  starting transfers between devices: 17.4 us -> 0 us
  between operations: 10.3 us -> 0.65 us
    pallas_call x0 -> x1, Pallas kernels: none -> 166 us  [local(): pl.pallas_call(functools.partial(kernel, n, chunks), out_shape=(shape, sh...]
    psum x2 -> x0, blocking collectives: 148 us -> none  [paired_sums(): lax.psum((jnp.sum(residual * precond), jnp.sum(image * precond)), 'gz')]
    pmax x1 -> x0, blocking collectives: 77.7 us -> none  [local(): fastest = lax.pmax(local_fastest, 'gz')]
    slice x13 -> x0, local copies, waits for them, and re-layouts: 51.6 us -> none  [the longest x8 36 us: later_cells(): tail = lax.slice_in_dim(field, 1, size, axis=axis)]
    mul x3 -> x0, other arithmetic: 43.3 us -> none  [the longest x2 36.5 us: apply_operator(): masked = search * fluid_cells]
    reduce_sum x2 -> x0, other arithmetic: 29.9 us -> none  [the longest x1 16.2 us: paired_sums(): jnp.sum(image * precond)]
    ppermute x7 -> x0, starting transfers between devices: 17.4 us -> none  [the longest x3 11.8 us: with_halo(): lax.ppermute(lax.slice_in_dim(block, block.shape[dim] - width, None, axis...]
  transfers between devices with their start and end apart: 7 -> 0, of which waited for: 0 -> 0; matrix products, arithmetic and copies ran while one was open for 10% -> 0% of each run, Pallas kernels for 0% -> 0%
where the time goes in v1:
time: 174 us; the launch traced here: 173 us
  Pallas kernels  166 us (95%)
  local copies, waits for them, and re-layouts  6.84 us (4%)
    pallas_call x1, Pallas kernels, local(): pl.pallas_call(functools.partial(kernel, n, chunks), out_shape=(shape, sh...  166 us
    unnamed x4, local copies, waits for them, and re-layouts  6.84 us

profile of v1, /device:TPU:0, one launch (start us, length us, event | category | flops | bytes accessed | tf_op | source)
XLA Modules:
  0.0 173.4 jit_solution(14948274600555584943)
XLA Ops:
  0.6 165.9 %smoke_step.1 = (f32[2,1024,512]{2,1,0:T(8,128)}, f32[2,1024,512]{2,1,0:T(8,128)}) custom-call(f32[2,1024,512]{2,1,0:T(8,128)} %u_hbm.1, f32[2,1024,512]{2,1,0:T(8,128)} %v_hbm.1, f32[2,1024,512]{2,1,0:T(8,128)} %w_hbm.1, f32[2,1024,512]{2,1,0:T(8,128)} %s_hbm.1, s32[2,32,512]{2,1,0:T(8,128)} %ob_hbm.1), custom_call_target="tpu_custom_call" | custom-call | tf_op jit(solution)/shard_map/smoke_step/pallas_call | solution.py:417
  166.5 0.0 copy-start
  166.6 4.8 %copy.9 = f32[2,1024,512]{2,1,0:T(8,128)} copy(f32[2,1024,512]{2,1,0:T(8,128)} %get-tuple-element.4) | data formatting | bytes 8388608
  171.4 0.0 copy-done
  171.4 2.0 %copy.10 = f32[2,1024,512]{2,1,0:T(8,128)} copy(f32[2,1024,512]{2,1,0:T(8,128)S(1)} %copy-done) | data formatting | bytes 8388608
Async XLA Ops:
  166.5 4.8 %copy-start = (f32[2,1024,512]{2,1,0:T(8,128)S(1)}, f32[2,1024,512]{2,1,0:T(8,128)}, u32[]{:S(2)}) copy-start(f32[2,1024,512]{2,1,0:T(8,128)} %get-tuple-element.5) | copy-start | bytes 12582916

commit v2 on v1

--- a/solution.py
+++ b/solution.py
@@ -184,8 +184,6 @@
                     bits[3] == 1, -1, 6 - count).astype(jnp.float32)
         return carry
 
-    lax.fori_loop(0, nb, code_rows, 0)
-
     for p in range(depth):
         load(3, p).wait()
     mx_wait()
@@ -216,7 +214,7 @@
                 for cond, copy in sends:
                     @pl.when(cond)
                     def _(copy=copy):
-                        copy(c - 1).start()
+                        copy(c - 1)
             return carry
         lax.fori_loop(0, chunks + 1, body, 0)
 
@@ -228,7 +226,8 @@
     def lw_rows(r):
         lw[0, pl.ds(r, ROWS), :] = lifted(0, r)
 
-    chunked(lambda c: None, lw_rows, [(has_low, lw_copy)])
+    chunked(lambda c: None, lw_rows, [(has_low, lambda c: lw_copy(c).start())])
+    lax.fori_loop(0, nb, code_rows, 0)
 
     def z_copy(src, dst, send, recv, base, device):
         def copy(c):
@@ -253,18 +252,25 @@
         z[p + 2, pl.ds(pl.multiple_of(r + PAD, 8), ROWS), :] = (
             jnp.where(k >= 0.0, div, 0.0) / jnp.maximum(k, 1.0))
 
-    for p in range(depth):
-        def prepare(c, p=p):
-            if p == depth - 1:
-                @pl.when(has_high)
-                def _():
-                    lw_copy(c).wait_recv()
-        sends = []
-        if p < 2:
-            sends.append((has_low, down[p]))
-        if p >= depth - 2:
-            sends.append((has_high, up[p - (depth - 2)]))
-        chunked(prepare, functools.partial(z_rows, p), sends)
+    def gated(before, copy):
+        def start(c):
+            before(c).wait_send()
+            copy(c).start()
+        return start
+
+    top_plane = [] if depth > 2 else [(has_high, lambda c: up[0](c).start())]
+    chunked(lambda c: None, functools.partial(z_rows, 0), top_plane)
+    for p in range(1, depth - 1):
+        sends = [(has_high, lambda c: up[0](c).start())] if p == depth - 2 else []
+        chunked(lambda c: None, functools.partial(z_rows, p), sends)
+
+    def above_wait(c):
+        @pl.when(has_high)
+        def _():
+            lw_copy(c).wait_recv()
+
+    chunked(above_wait, functools.partial(z_rows, depth - 1),
+            [(has_high, gated(up[0], up[1])), (has_low, gated(lw_copy, down[0]))])
 
     def wait_all(cond, copy):
         def body(c, carry):
@@ -314,27 +320,60 @@
             return carry
         lax.fori_loop(0, nb, body, 0)
 
+    for p in range(1, depth - 1):
+        sweep(functools.partial(y_rows, p))
     wait_all(has_low, up[0])
-    for p in range(depth - 1):
-        if p == 0:
-            wait_all(has_low, up[1])
-            sweep(functools.partial(y_rows, -1))
-        sweep(functools.partial(y_rows, p))
-    wait_all(has_high, down[0])
-    sweep(functools.partial(y_rows, depth - 1))
-    for p in range(depth - 1):
-        sweep(functools.partial(a_rows, p))
-
-    def last_wait(c):
-        @pl.when(has_high)
-        def _():
-            down[1](c).wait_recv()
-
-    def last_rows(r):
-        y_rows(depth, r)
-        a_rows(depth - 1, r)
-
-    chunked(last_wait, last_rows, [])
+
+    def push(c, carry):
+        @pl.when(has_low)
+        def _():
+            gated(down[0], down[1])(c)
+        return carry
+
+    lax.fori_loop(0, chunks, push, 0)
+
+    def middle(c, carry):
+        def over(c, fn):
+            def inner(i, k):
+                fn(pl.multiple_of(c * crow + i * ROWS, 8))
+                return k
+            lax.fori_loop(0, crow // ROWS, inner, 0)
+
+        def ahead(r):
+            for p in sorted({0, depth - 1, depth}):
+                y_rows(p, r)
+
+        def behind(r):
+            y_rows(-1, r)
+            for p in range(depth):
+                a_rows(p, r)
+
+        @pl.when(c < chunks)
+        def _():
+            @pl.when(has_low)
+            def _():
+                up[1](c).wait_recv()
+
+            @pl.when(has_high)
+            def _():
+                down[1](c).wait_recv()
+
+                @pl.when(c == 0)
+                def _():
+                    down[0](0).wait_recv()
+
+                @pl.when(c + 1 < chunks)
+                def _():
+                    down[0](c + 1).wait_recv()
+
+            over(c, ahead)
+
+        @pl.when(c > 0)
+        def _():
+            over(c - 1, behind)
+        return carry
+
+    lax.fori_loop(0, chunks + 1, middle, 0)
 
     for j in range(6):
         t = jnp.sum(acc[j], axis=0, keepdims=True)
@@ -349,13 +388,10 @@
     def drain(c, carry):
         @pl.when(has_low)
         def _():
-            lw_copy(c).wait_send()
-            down[0](c).wait_send()
             down[1](c).wait_send()
 
         @pl.when(has_high)
         def _():
-            up[0](c).wait_send()
             up[1](c).wait_send()
         return carry
 
@@ -392,7 +428,7 @@
             s[p, rows, :] = (scaling * (zz - a * yy) + b * ay[p, rows, :]) * cf[3:4, :]
 
         chunked(lambda c: None, out_rows,
-                [(True, lambda c, p=p: out_copy(p, c, 0)), (True, lambda c, p=p: out_copy(p, c, 1))])
+                [(True, lambda c, p=p: out_copy(p, c, 0).start()), (True, lambda c, p=p: out_copy(p, c, 1).start())])
 
     def finish(c, carry):
         for p in range(depth):

time: 174 us -> 151 us (0.87)
  Pallas kernels: 166 us -> 144 us
    pallas_call x1, Pallas kernels: 166 us -> 144 us  [local(): pl.pallas_call(functools.partial(kernel, n, chunks), out_shape=(shape, sh...]
where the time goes in v2:
time: 151 us
  Pallas kernels  144 us (95%)
  local copies, waits for them, and re-layouts  6.84 us (5%)
    pallas_call x1, Pallas kernels, local(): pl.pallas_call(functools.partial(kernel, n, chunks), out_shape=(shape, sh...  144 us
    unnamed x4, local copies, waits for them, and re-layouts  6.84 us

profile of v2, /device:TPU:0, one launch (start us, length us, event | category | flops | bytes accessed | tf_op | source)
XLA Modules:
  0.0 151.2 jit_solution(1673391535186870036)
XLA Ops:
  0.6 143.7 %smoke_step.1 = (f32[2,1024,512]{2,1,0:T(8,128)}, f32[2,1024,512]{2,1,0:T(8,128)}) custom-call(f32[2,1024,512]{2,1,0:T(8,128)} %u_hbm.1, f32[2,1024,512]{2,1,0:T(8,128)} %v_hbm.1, f32[2,1024,512]{2,1,0:T(8,128)} %w_hbm.1, f32[2,1024,512]{2,1,0:T(8,128)} %s_hbm.1, s32[2,32,512]{2,1,0:T(8,128)} %ob_hbm.1), custom_call_target="tpu_custom_call" | custom-call | tf_op jit(solution)/shard_map/smoke_step/pallas_call | solution.py:453
  144.3 0.0 copy-start
  144.3 4.8 %copy.9 = f32[2,1024,512]{2,1,0:T(8,128)} copy(f32[2,1024,512]{2,1,0:T(8,128)} %get-tuple-element.4) | data formatting | bytes 8388608
  149.2 0.0 copy-done
  149.2 2.0 %copy.10 = f32[2,1024,512]{2,1,0:T(8,128)} copy(f32[2,1024,512]{2,1,0:T(8,128)S(1)} %copy-done) | data formatting | bytes 8388608
Async XLA Ops:
  144.3 4.8 %copy-start = (f32[2,1024,512]{2,1,0:T(8,128)S(1)}, f32[2,1024,512]{2,1,0:T(8,128)}, u32[]{:S(2)}) copy-start(f32[2,1024,512]{2,1,0:T(8,128)} %get-tuple-element.5) | copy-start | bytes 12582916

commit v3 on v2

--- a/solution.py
+++ b/solution.py
@@ -15,7 +15,7 @@
 PAD = 8
 
 
-def kernel(n, chunks, u_hbm, v_hbm, w_hbm, s_hbm, ob_hbm, imp_hbm, res_hbm,
+def kernel(n, chunks, u_hbm, v_hbm, w_hbm, s_hbm, ob_hbm, z_out, y_out, code_out, ay_out, cf_out,
            u, v, w, s, z, y, code, ay, lw, lw_next, ob, cw, acc, cf, mx, mx_all, st, st_all,
            in_sem, ob_send, ob_recv, lw_send, lw_recv, dn_send, dn_recv, up_send, up_recv,
            mx_send, mx_recv, st_send, st_recv, out_sem):
@@ -59,6 +59,7 @@
     for p in range(depth):
         v[p, ny : ny + PAD, :] = zrow
     acc[...] = jnp.zeros_like(acc)
+    cf[...] = jnp.zeros_like(cf)
 
     def zero_planes(ref, planes, offset):
         def body(i, carry):
@@ -385,6 +386,16 @@
     st_start, st_wait = spread(st, st_all, st_send, st_recv)
     st_start()
 
+    inner = pl.ds(PAD, ny)
+    outs = [
+        pltpu.make_async_copy(z.at[pl.ds(2, depth), inner], z_out, out_sem.at[0]),
+        pltpu.make_async_copy(y.at[pl.ds(1, depth), inner], y_out, out_sem.at[1]),
+        pltpu.make_async_copy(code.at[pl.ds(1, depth)], code_out, out_sem.at[2]),
+        pltpu.make_async_copy(ay, ay_out, out_sem.at[3]),
+    ]
+    for copy in outs:
+        copy.start()
+
     def drain(c, carry):
         @pl.when(has_low)
         def _():
@@ -412,31 +423,11 @@
     cf[2:3, :] = alpha * alpha_next
     cf[3:4, :] = 1.0 / jnp.sqrt(squares / jnp.maximum(fluid, 1.0) + EPS)
 
-    def out_copy(p, c, j):
-        rows = pl.ds(pl.multiple_of(c * crow, 8), crow)
-        src, dst = ((w, imp_hbm), (s, res_hbm))[j]
-        return pltpu.make_async_copy(src.at[p, rows], dst.at[p, rows], out_sem.at[j * depth + p, c])
-
-    for p in range(depth):
-        def out_rows(r, p=p):
-            inner = pl.ds(pl.multiple_of(r + PAD, 8), ROWS)
-            rows = pl.ds(r, ROWS)
-            zz, yy = z[p + 2, inner, :], y[p + 1, inner, :]
-            scaling = jnp.maximum(code[p + 1, rows, :], 1.0)
-            a, b = cf[1:2, :], cf[2:3, :]
-            w[p, rows, :] = a * zz - b * yy
-            s[p, rows, :] = (scaling * (zz - a * yy) + b * ay[p, rows, :]) * cf[3:4, :]
-
-        chunked(lambda c: None, out_rows,
-                [(True, lambda c, p=p: out_copy(p, c, 0).start()), (True, lambda c, p=p: out_copy(p, c, 1).start())])
-
-    def finish(c, carry):
-        for p in range(depth):
-            for j in range(2):
-                out_copy(p, c, j).wait()
-        return carry
-
-    lax.fori_loop(0, chunks, finish, 0)
+    cf_copy = pltpu.make_async_copy(cf, cf_out, out_sem.at[4])
+    cf_copy.start()
+    cf_copy.wait()
+    for copy in outs:
+        copy.wait()
 
 
 def solution(mesh):
@@ -450,11 +441,11 @@
         dma = pltpu.SemaphoreType.DMA
         any_spec = pl.BlockSpec(memory_space=pl.ANY)
         shape = jax.ShapeDtypeStruct((depth, ny, nx), f32)
-        return pl.pallas_call(
+        z, y, code, ay, cf = pl.pallas_call(
             functools.partial(kernel, n, chunks),
-            out_shape=(shape, shape),
+            out_shape=(shape,) * 4 + (jax.ShapeDtypeStruct((8, nx), f32),),
             in_specs=[any_spec] * 5,
-            out_specs=(any_spec, any_spec),
+            out_specs=(any_spec,) * 5,
             scratch_shapes=[
                 pltpu.VMEM((depth, ny, nx), f32),
                 pltpu.VMEM((depth, ny + PAD, nx), f32),
@@ -481,12 +472,16 @@
                 dma((2 * chunks,)), dma((2 * chunks,)),
                 dma((n,)), dma((n,)),
                 dma((n,)), dma((n,)),
-                dma((2 * depth, chunks)),
+                dma((5,)),
             ],
             compiler_params=pltpu.CompilerParams(
                 collective_id=0, has_side_effects=True, vmem_limit_bytes=66_000_000),
             name="smoke_step",
         )(u_face, v_face, w_face, smoke, obstacles)
+        a, b, norm = cf[1, 0], cf[2, 0], cf[3, 0]
+        impulse = a * z - b * y
+        residual = (jnp.maximum(code, 1.0) * (z - a * y) + b * ay) * norm
+        return impulse, residual
 
     placed = P("gz", None, None)
     return jax.shard_map(local, mesh=mesh, in_specs=(placed,) * 5, out_specs=(placed, placed), check_vma=False)

time: 151 us -> 157 us (1.040); the launches traced: 151 us -> 154 us
  other arithmetic: 0 us -> 11.5 us
  local copies, waits for them, and re-layouts: 6.84 us -> 1.38 us
  Pallas kernels: 144 us -> 141 us
    mul x0 -> x1, other arithmetic: none -> 11.5 us  [local(): residual = (jnp.maximum(code, 1.0) * (z - a * y) + b * ay) * norm]
    unnamed x4 -> x0, local copies, waits for them, and re-layouts: 6.84 us -> none
    pallas_call x1, Pallas kernels: 144 us -> 141 us  [local(): pl.pallas_call(functools.partial(kernel, n, chunks), out_shape=(shape,) *...]
where the time goes in v3:
time: 157 us; the launch traced here: 154 us
  Pallas kernels  141 us (90%)
  other arithmetic  11.5 us (7%)
    pallas_call x1, Pallas kernels, local(): pl.pallas_call(functools.partial(kernel, n, chunks), out_shape=(shape,) *...  141 us
    mul x1, other arithmetic, local(): residual = (jnp.maximum(code, 1.0) * (z - a * y) + b * ay) * norm  11.5 us

profile of v3, /device:TPU:0, one launch (start us, length us, event | category | flops | bytes accessed | tf_op | source)
XLA Modules:
  0.0 154.2 jit_solution(967087060759097974)
XLA Ops:
  0.6 140.7 %smoke_step.1 = (f32[2,1024,512]{2,1,0:T(8,128)}, f32[2,1024,512]{2,1,0:T(8,128)}, f32[2,1024,512]{2,1,0:T(8,128)}, f32[2,1024,512]{2,1,0:T(8,128)}, f32[8,512]{1,0:T(8,128)}) custom-call(f32[2,1024,512]{2,1,0:T(8,128)} %u_hbm.1, f32[2,1024,512]{2,1,0:T(8,128)} %v_hbm.1, f32[2,1024,512]{2,1,0:T(8,128)} %w_hbm.1, f32[2,1024,512]{2,1,0:T(8,128)} %s_hbm.1, ...), custom_call_target="tpu_custom_call" | custom-call | tf_op jit(solution)/shard_map/smoke_step/pallas_call | solution.py:444
  141.3 1.4 fusion
  142.7 11.5 %add_multiply_fusion = (f32[2,1024,512]{2,1,0:T(8,128)}, f32[2,1024,512]{2,1,0:T(8,128)}) fusion(f32[2,1024,512]{2,1,0:T(8,128)} %get-tuple-element.11, f32[2,1024,512]{2,1,0:T(8,128)} %get-tuple-element.8, f32[2,1024,512]{2,1,0:T(8,128)} %get-tuple-element.9, f32[2,1024,512]{2,1,0:T(8,128)} %get-tuple-element.10, f32[]{:T(128)} %bitcast.2, f32[]{:T(128)} %bitcast.1, ...), kind=kLoop, calls=%fused_computation | loop fusion | flops 10485760 | bytes 25165836 | tf_op jit(solution)/shard_map/mul | solution.py:483
